TPU v7x, 256 devices: a whole 4x4x8 slice. The times are simulated.
256 devices in a mesh: bins: 16 (over x, z_lo, core), sta: 16 (over z_hi, y).
Axes of the slice: x: 4, y: 4, z: 8 (z_hi: 4, z_lo: 2; z = z_hi * 2 + z_lo), core: 2. Of those that a mesh axis runs over, the one named last changes fastest.
Arguments:
- spectra: bfloat16 [2, 128, 8, 4096], P(None, 'bins', None, 'sta'), may hold values from -110 to 110
- coords: int32 [2, 4096], replicated, may hold values from 0 to 2047
- slowness: int32 [2, 2048], replicated, may hold values from -32 to 31
Outputs:
- beam_power: float32 [128, 2048], P('bins', 'sta')
All inputs are finite; a program needn't handle non-finite values.
Results may differ from a plain program's by a relative error of at most 0.002.
Values may be sent and summed in bfloat16 or wider, within the bound.
A program may use at most 64 MiB of HBM per device.

v0:
```python
import math

import jax
import jax.numpy as jnp
from jax import lax
from jax.sharding import PartitionSpec as P

phase_modulus = 1048576
two_pi = 2.0 * math.pi
epsilon = 1e-06


def sent_to_all(x, axis):
    peers = lax.axis_size(axis)
    return lax.all_to_all(jnp.broadcast_to(x[None], (peers, *x.shape)), axis, 0, 0, tiled=True)


def of_everyone(x, axis):
    return sent_to_all(x, axis).sum(axis=0)


def joined_along(blocks, dim):
    blocks = jnp.moveaxis(blocks, 0, dim)
    lengths = blocks.shape
    return blocks.reshape(*lengths[:dim], lengths[dim] * lengths[dim + 1], *lengths[dim + 2 :])


def collect(x, axis, dim):
    return joined_along(sent_to_all(x, axis), dim)


def steering_table(delays, bin_number):
    phase_index = jnp.mod(bin_number * delays, phase_modulus)
    phase = phase_index.astype(jnp.float32) * (two_pi / phase_modulus)
    return jnp.concatenate([jnp.cos(phase), jnp.sin(phase)], 0).astype(jnp.bfloat16)


def stack_rows(whitened):
    real_part = whitened[0]
    imag_part = whitened[1]
    upper_rows = jnp.concatenate([real_part, imag_part], 2)
    bottom = jnp.concatenate([imag_part, -real_part], 2)
    return jnp.concatenate([upper_rows, bottom], 1)


def beam_terms(stacked, bin_numbers, coords_part, slow_part):
    row_count = slow_part.shape[1]
    block_size = math.gcd(row_count, 256)
    block_count = row_count // block_size
    groups = jnp.transpose(slow_part.reshape(2, block_count, block_size), (1, 0, 2))

    def one_block(slow_block):
        delays = (
            slow_block[0][None, :] * coords_part[0][:, None]
            + slow_block[1][None, :] * coords_part[1][:, None]
        )

        def one_bin(pair_args):
            bin_rows, bin_number = pair_args
            steering = steering_table(delays, bin_number)
            return lax.dot_general(
                steering, bin_rows, (((0,), (1,)), ((), ())), preferred_element_type=jnp.float32
            )

        amps = lax.map(one_bin, (stacked, bin_numbers))
        return jnp.transpose(amps, (1, 0, 2)).reshape(block_size, -1)

    blocks = lax.map(one_block, groups)
    return blocks.reshape(row_count, -1)


def local(spectra, coords, slowness):
    bins_dev = spectra.shape[1]
    seg_count = spectra.shape[2]
    values = spectra.astype(jnp.float32)
    local_sq = jnp.sum(values * values, axis=(0, 1))
    total_bins = bins_dev * lax.axis_size("bins")
    totals = of_everyone(local_sq, "bins")
    scale = jnp.sqrt(totals / (2 * total_bins) + epsilon)
    whitened = (values / scale).astype(jnp.bfloat16)
    bin_numbers = lax.axis_index("bins") * bins_dev + 1 + jnp.arange(bins_dev, dtype=jnp.int32)
    stations = coords.shape[1]
    beam_count = slowness.shape[1]
    beams_dev = beam_count // lax.axis_size("sta")
    own_index = lax.axis_index("sta")
    own_beams = lax.dynamic_slice_in_dim(slowness, own_index * beams_dev, beams_dev, 1)
    amplitude = beam_terms(stack_rows(collect(whitened, "sta", 3)), bin_numbers, coords, own_beams)
    amplitude = amplitude.reshape(beams_dev, bins_dev, 2 * seg_count)
    beam_power = jnp.sum(amplitude * amplitude, axis=2).T / (stations * seg_count)
    return beam_power


def solution(mesh):
    in_specs = (P(None, "bins", None, "sta"), P(), P())
    out_specs = P("bins", "sta")
    return jax.shard_map(local, mesh=mesh, in_specs=in_specs, out_specs=out_specs, check_vma=False)
```

profile of v0, /device:TPU:1, one launch (start us, length us, event | category | flops | bytes accessed | tf_op | source)
XLA Modules:
  0.0 145.9 jit_solution(2820585037216760672)
XLA Ops:
  0.0 0.9 fusion.19
  0.9 13.1 %all_to_all.10 = f32[16,8,256]{2,1,0:T(8,128)S(1)} all-to-all(f32[16,8,256]{2,1,0:T(8,128)S(1)} %broadcast_in_dim.24), channel_id=1, replica_groups=mesh['bins'=16,'sta'=16] {'bins'}, dimensions={0} | all-to-all | bytes 262144 | tf_op jit(solution)/shard_map/all_to_all | solution.py:15
  14.0 0.9 fusion.20
  14.9 1.1 broadcast_in_dim.25
  16.0 10.0 %all-to-all-start.1 = ((bf16[16,2,8,8,256]{4,3,2,1,0:T(8,128)(2,1)}), bf16[16,2,8,8,256]{4,3,2,1,0:T(8,128)(2,1)S(1)}, u32[]{:S(2)}, u32[]{:S(2)}) async-start(bf16[16,2,8,8,256]{4,3,2,1,0:T(8,128)(2,1)} %broadcast_in_dim.25), calls=%async_computation.1 | async-start | bytes 2097152 | tf_op jit(solution)/shard_map/all_to_all | solution.py:15
  26.1 27.5 %all-to-all-done.1 = bf16[16,2,8,8,256]{4,3,2,1,0:T(8,128)(2,1)S(1)} async-done(((bf16[16,2,8,8,256]{4,3,2,1,0:T(8,128)(2,1)}), bf16[16,2,8,8,256]{4,3,2,1,0:T(8,128)(2,1)S(1)}, u32[]{:S(2)}, u32[]{:S(2)}) %all-to-all-start.1) | async-done | bytes 1048608 | tf_op jit(solution)/shard_map/all_to_all | solution.py:15
  54.7 1.0 squeeze.28
  55.7 1.4 maximum_maximum_fusion
  57.0 88.3 %while.20 = (s32[]{:T(128)}, f32[8,128,16]{1,2,0:T(8,128)S(1)}, s32[8]{0:T(128)S(1)}, bf16[8,16,8192]{2,1,0:T(8,128)(2,1)S(1)}, s32[4096]{0:T(1024)S(1)}, /*inde...) while((s32[]{:T(128)}, f32[8,128,16]{1,2,0:T(8,128)S(1)}, s32[8]{0:T(128)S(1)}, ...), condition=%wide.region_3.4_spmd.clone, body=%wide.region_2.3_spmd.clone.sunk | while | flops 47710208 | bytes 4499565 | solution.py:65
  57.6 10.0 %cosine_convert_fusion.2 = (bf16[4096,128]{1,0:T(8,128)(2,1)S(1)}, bf16[4096,128]{1,0:T(8,128)(2,1)S(1)}) fusion(s32[4096]{0:T(1024)S(1)} %get-tuple-element.213, s32[128]{0:T(128)S(1)} %get-tuple-element.214, s32[4096]{0:T(1024)S(1)} %get-tuple-element.211, s32[128]{0:T(128)S(1)} %get-tuple-element.212, s32[]{:T(128)} %bitcast.24), kind=kLoop, calls=%fused_computation.13.clone.1 | loop fusion | flops 9961472 | bytes 2130948 | tf_op jit(solution)/shard_map/convert
  68.1 0.6 dynamic_slice.31
  68.7 10.0 %cosine_convert_fusion.2 = (bf16[4096,128]{1,0:T(8,128)(2,1)S(1)}, bf16[4096,128]{1,0:T(8,128)(2,1)S(1)}) fusion(s32[4096]{0:T(1024)S(1)} %get-tuple-element.213, s32[128]{0:T(128)S(1)} %get-tuple-element.214, s32[4096]{0:T(1024)S(1)} %get-tuple-element.211, s32[128]{0:T(128)S(1)} %get-tuple-element.212, s32[]{:T(128)} %bitcast.24), kind=kLoop, calls=%fused_computation.13.clone.1 | loop fusion | flops 9961472 | bytes 2130948 | tf_op jit(solution)/shard_map/convert
  79.1 0.6 dynamic_slice.31
  79.7 10.0 %cosine_convert_fusion.2 = (bf16[4096,128]{1,0:T(8,128)(2,1)S(1)}, bf16[4096,128]{1,0:T(8,128)(2,1)S(1)}) fusion(s32[4096]{0:T(1024)S(1)} %get-tuple-element.213, s32[128]{0:T(128)S(1)} %get-tuple-element.214, s32[4096]{0:T(1024)S(1)} %get-tuple-element.211, s32[128]{0:T(128)S(1)} %get-tuple-element.212, s32[]{:T(128)} %bitcast.24), kind=kLoop, calls=%fused_computation.13.clone.1 | loop fusion | flops 9961472 | bytes 2130948 | tf_op jit(solution)/shard_map/convert
  90.1 0.6 dynamic_slice.31
  90.7 10.0 %cosine_convert_fusion.2 = (bf16[4096,128]{1,0:T(8,128)(2,1)S(1)}, bf16[4096,128]{1,0:T(8,128)(2,1)S(1)}) fusion(s32[4096]{0:T(1024)S(1)} %get-tuple-element.213, s32[128]{0:T(128)S(1)} %get-tuple-element.214, s32[4096]{0:T(1024)S(1)} %get-tuple-element.211, s32[128]{0:T(128)S(1)} %get-tuple-element.212, s32[]{:T(128)} %bitcast.24), kind=kLoop, calls=%fused_computation.13.clone.1 | loop fusion | flops 9961472 | bytes 2130948 | tf_op jit(solution)/shard_map/convert
  101.2 0.6 dynamic_slice.31
  101.8 10.0 %cosine_convert_fusion.2 = (bf16[4096,128]{1,0:T(8,128)(2,1)S(1)}, bf16[4096,128]{1,0:T(8,128)(2,1)S(1)}) fusion(s32[4096]{0:T(1024)S(1)} %get-tuple-element.213, s32[128]{0:T(128)S(1)} %get-tuple-element.214, s32[4096]{0:T(1024)S(1)} %get-tuple-element.211, s32[128]{0:T(128)S(1)} %get-tuple-element.212, s32[]{:T(128)} %bitcast.24), kind=kLoop, calls=%fused_computation.13.clone.1 | loop fusion | flops 9961472 | bytes 2130948 | tf_op jit(solution)/shard_map/convert
  112.2 0.6 dynamic_slice.31
  112.8 10.0 %cosine_convert_fusion.2 = (bf16[4096,128]{1,0:T(8,128)(2,1)S(1)}, bf16[4096,128]{1,0:T(8,128)(2,1)S(1)}) fusion(s32[4096]{0:T(1024)S(1)} %get-tuple-element.213, s32[128]{0:T(128)S(1)} %get-tuple-element.214, s32[4096]{0:T(1024)S(1)} %get-tuple-element.211, s32[128]{0:T(128)S(1)} %get-tuple-element.212, s32[]{:T(128)} %bitcast.24), kind=kLoop, calls=%fused_computation.13.clone.1 | loop fusion | flops 9961472 | bytes 2130948 | tf_op jit(solution)/shard_map/convert
  123.2 0.6 dynamic_slice.31
  123.8 10.0 %cosine_convert_fusion.2 = (bf16[4096,128]{1,0:T(8,128)(2,1)S(1)}, bf16[4096,128]{1,0:T(8,128)(2,1)S(1)}) fusion(s32[4096]{0:T(1024)S(1)} %get-tuple-element.213, s32[128]{0:T(128)S(1)} %get-tuple-element.214, s32[4096]{0:T(1024)S(1)} %get-tuple-element.211, s32[128]{0:T(128)S(1)} %get-tuple-element.212, s32[]{:T(128)} %bitcast.24), kind=kLoop, calls=%fused_computation.13.clone.1 | loop fusion | flops 9961472 | bytes 2130948 | tf_op jit(solution)/shard_map/convert
  134.9 10.0 %cosine_convert_fusion.2 = (bf16[4096,128]{1,0:T(8,128)(2,1)S(1)}, bf16[4096,128]{1,0:T(8,128)(2,1)S(1)}) fusion(s32[4096]{0:T(1024)S(1)} %get-tuple-element.213, s32[128]{0:T(128)S(1)} %get-tuple-element.214, s32[4096]{0:T(1024)S(1)} %get-tuple-element.211, s32[128]{0:T(128)S(1)} %get-tuple-element.212, s32[]{:T(128)} %bitcast.24), kind=kLoop, calls=%fused_computation.13.clone.1 | loop fusion | flops 9961472 | bytes 2130948 | tf_op jit(solution)/shard_map/convert
  145.3 0.6 broadcast_multiply_fusion
  (28 shorter events, 5.5 us)
Async XLA Ops:
  0.0 26.0 %copy-start = (s32[2,2048]{1,0:T(2,128)S(1)}, s32[2,2048]{1,0:T(2,128)}, u32[]{:S(2)}) copy-start(s32[2,2048]{1,0:T(2,128)} %param.7) | copy-start | bytes 49156
  0.0 26.1 %copy-start.1 = (s32[2,4096]{1,0:T(2,128)S(1)}, s32[2,4096]{1,0:T(2,128)}, u32[]{:S(2)}) copy-start(s32[2,4096]{1,0:T(2,128)} %param.6) | copy-start | bytes 98308
  16.0 37.6 %all-to-all-start.1 = ((bf16[16,2,8,8,256]{4,3,2,1,0:T(8,128)(2,1)}), bf16[16,2,8,8,256]{4,3,2,1,0:T(8,128)(2,1)S(1)}, u32[]{:S(2)}, u32[]{:S(2)}) async-start(bf16[16,2,8,8,256]{4,3,2,1,0:T(8,128)(2,1)} %broadcast_in_dim.25), calls=%async_computation.1 | async-start | bytes 2097152 | tf_op jit(solution)/shard_map/all_to_all | solution.py:15
where the time goes:
time: 147 us; the launch traced here: 146 us
  other arithmetic  84.1 us (57%)
  waiting for transfers between devices  27.5 us (19%)
  blocking collectives  13.1 us (9%)
  starting transfers between devices  10 us (7%)
  local copies, waits for them, and re-layouts  7.81 us (5%)
  matrix products  3.16 us (2%)
    another operation x9, other arithmetic  80.3 us
    all_to_all x1, waiting for transfers between devices, sent_to_all(): lax.all_to_all(jnp.broadcast_to(x[None], (peers, *x.shape)), axis, 0, 0,...  27.5 us
    all_to_all x1, blocking collectives, sent_to_all(): lax.all_to_all(jnp.broadcast_to(x[None], (peers, *x.shape)), axis, 0, 0,...  13.1 us
    all_to_all x1, starting transfers between devices, sent_to_all(): lax.all_to_all(jnp.broadcast_to(x[None], (peers, *x.shape)), axis, 0, 0,...  10 us
    dynamic_slice x8, local copies, waits for them, and re-layouts, one_block(): amps = lax.map(one_bin, (stacked, bin_numbers))  4.69 us
    dot_general x8, matrix products, one_bin(): lax.dot_general(steering, bin_rows, (((0,), (1,)), ((), ())), preferred_e...  3.16 us
  transfers between devices with their start and end apart: 1, of which 1 were waited for; matrix products, arithmetic and copies ran while one was open for 0% of the time, Pallas kernels for 0%

commit v1 on v0

v1 whole, which is shorter than its diff:
```python
import math

import jax
import jax.numpy as jnp
import numpy as np
from jax import lax
from jax.experimental import pallas as pl
from jax.experimental.pallas import tpu as pltpu
from jax.sharding import PartitionSpec as P

MESH = pl.DeviceIdType.MESH
epsilon = 1e-06
GRID_K = 32
N_BINS = 16
N_STA = 16


def cheb_fit(fn, degree):
    nodes = np.cos(np.pi * (np.arange(4001) + 0.5) / 4001)
    u = (nodes + 1.0) / 2.0
    return np.polynomial.chebyshev.Chebyshev.fit(u, fn(u), degree, domain=[0, 1]).convert(
        kind=np.polynomial.Polynomial
    ).coef


def cos_coefs():
    return [float(c) for c in cheb_fit(lambda u: np.cos(np.pi * np.sqrt(u)), 7)]


def sin_coefs():
    return [float(c) for c in cheb_fit(lambda u: np.pi * np.sinc(np.sqrt(u)), 6)]


COS = cos_coefs()
SIN = sin_coefs()


def horner(coefs, u):
    acc = jnp.full_like(u, coefs[-1])
    for c in coefs[-2::-1]:
        acc = acc * u + c
    return acc


def cos_sin(index):
    t = lax.shift_right_arithmetic(lax.shift_left(index, 11), 11).astype(jnp.float32) * (1.0 / 1048576)
    u = t * t
    return horner(COS, u), horner(SIN, u) * t


def kernel(
    x_hbm, co_hbm, sl_hbm, out_ref,
    xv, cov, slv, raw_send, raw_recv, part_send, part_recv, r_send, r_recv, pow_send, pow_recv,
    tabx, taby, xrot, wbuf, pick,
    in_sem, part_ss, part_rs, raw_ss, raw_rs, r_ss, r_rs, pow_ss, pow_rs,
):
    bi = lax.axis_index("bins")
    sj = lax.axis_index("sta")
    core = bi % 2
    chip = bi - core
    half = sj % 2
    f1 = bi * 8 + sj // 2 + 1

    loads = [
        pltpu.make_async_copy(src, dst, in_sem.at[n])
        for n, (src, dst) in enumerate(((x_hbm, xv), (co_hbm, cov), (sl_hbm, slv)))
    ]
    for load in loads:
        load.start()

    barrier = pltpu.get_barrier_semaphore()

    def greet_bins(d, _):
        pl.semaphore_signal(barrier, inc=1, device_id=((bi + d) % N_BINS, sj), device_id_type=MESH)
        return 0

    def greet_sta(d, _):
        q = (sj + d) % N_STA
        pl.semaphore_signal(barrier, inc=1, device_id=(bi, q), device_id_type=MESH)
        pl.semaphore_signal(barrier, inc=1, device_id=(chip + 1 - core, q), device_id_type=MESH)
        return 0

    lax.fori_loop(1, N_BINS, greet_bins, 0)
    lax.fori_loop(1, N_STA, greet_sta, 0)

    loads[0].wait()
    sq = jnp.zeros((8, 256), jnp.float32)
    for b in range(8):
        re = xv[0, b].astype(jnp.float32)
        im = xv[1, b].astype(jnp.float32)
        sq = sq + (re * re + im * im)
        for h in range(2):
            rows = slice(4 * h, 4 * h + 4)
            raw_send[2 * b + h] = jnp.concatenate(
                [re[rows, :128], im[rows, :128], re[rows, 128:], im[rows, 128:]], 0
            ).astype(jnp.bfloat16)
    for h in range(2):
        rows = slice(4 * h, 4 * h + 4)
        part_send[h] = jnp.concatenate([sq[rows, :128], sq[rows, 128:]], 0)

    pl.semaphore_wait(barrier, 45)

    def part_copy(d):
        p = (bi + d) % N_BINS
        return pltpu.make_async_remote_copy(
            src_ref=part_send.at[p % 2], dst_ref=part_recv.at[bi],
            send_sem=part_ss.at[p], recv_sem=part_rs.at[bi],
            device_id=(p, sj), device_id_type=MESH,
        )

    def raw_copy(d):
        q = (sj + d) % N_STA
        return pltpu.make_async_remote_copy(
            src_ref=raw_send.at[q], dst_ref=raw_recv.at[sj],
            send_sem=raw_ss.at[q], recv_sem=raw_rs.at[sj],
            device_id=(bi, q), device_id_type=MESH,
        )

    def r_copy(dc, e):
        q = ((sj // 2 + e) % 8) * 2 + core
        return pltpu.make_async_remote_copy(
            src_ref=r_send, dst_ref=r_recv.at[sj],
            send_sem=r_ss.at[dc * 8 + e], recv_sem=r_rs.at[sj],
            device_id=(chip + (core + dc) % 2, q), device_id_type=MESH,
        )

    def pow_copy(d):
        q = (sj + d) % N_STA
        return pltpu.make_async_remote_copy(
            src_ref=pow_send.at[q], dst_ref=pow_recv.at[sj],
            send_sem=pow_ss.at[q], recv_sem=pow_rs.at[sj],
            device_id=(bi, q), device_id_type=MESH,
        )

    def arrival(buf, sems, k):
        return pltpu.make_async_copy(buf.at[k], buf.at[k], sems.at[k])

    def loop(lo, hi, body):
        lax.fori_loop(lo, hi, lambda d, c: (body(d), c)[1], 0)

    loop(1, N_BINS, lambda d: part_copy(d).start())
    loop(1, N_STA, lambda d: raw_copy(d).start())
    part_recv[bi] = part_send[core]
    raw_recv[sj] = raw_send[sj]

    loads[1].wait()
    loads[2].wait()
    odd = lax.broadcasted_iota(jnp.int32, (GRID_K, 256), 0) * 2 + 1

    def tables(j):
        lanes = pl.ds(pl.multiple_of(j * 256, 256), 256)
        cx = cov[0:1, lanes] * f1
        cy = cov[1:2, lanes] * f1
        c, s = cos_sin(odd * cx)
        tabx[0, :, lanes] = c
        tabx[1, :, lanes] = s
        c, s = cos_sin(odd * cy)
        c = c.astype(jnp.bfloat16)
        s = s.astype(jnp.bfloat16)
        taby[:, lanes] = jnp.concatenate([c, c, s, s], 0)

    loop(0, 16, tables)

    def part_wait(d):
        p = (bi + d) % N_BINS
        arrival(part_recv, part_rs, p).wait()

    loop(1, N_BINS, part_wait)
    total = part_recv[0]
    for p in range(1, N_BINS):
        total = total + part_recv[p]
    inv = 1.0 / jnp.sqrt(total / 256.0 + epsilon)
    r_send[...] = inv
    loop(0, 8, lambda e: r_copy(1, e).start())
    loop(1, 8, lambda e: r_copy(0, e).start())

    @pl.when(half != core)
    def _():
        r_copy(0, 0).start()

    @pl.when(half == core)
    def _():
        r_recv[sj] = inv

    sx = slv[0:1, :]
    sy = slv[1:2, :]
    xneg = lax.shift_right_arithmetic(sx, 31)
    yneg = lax.shift_right_arithmetic(sy, 31)
    kx = sx ^ xneg
    ky = sy ^ yneg
    quad = jnp.where(sx >= 0, jnp.where(sy >= 0, 0, 32), jnp.where(sy >= 0, 96, 64))
    where_y = ky + quad
    for n in range(0, 2048, 256):
        hot = lax.broadcasted_iota(jnp.int32, (128, 256), 0) == where_y[:, n : n + 256]
        pick[:, n : n + 256] = jnp.where(hot, 1.0, 0.0).astype(jnp.bfloat16)

    loop(1, N_STA, lambda d: arrival(raw_recv, raw_rs, (sj + d) % N_STA).wait())
    sign = jnp.where(lax.broadcasted_iota(jnp.int32, (8, 256), 0) < 4, -1.0, 1.0)

    def rotate(j):
        lanes = pl.ds(pl.multiple_of(j * 256, 256), 256)
        raw = raw_recv[j].astype(jnp.float32)
        x = jnp.concatenate([raw[:8], raw[8:]], 1)
        swapped = jnp.concatenate([x[4:], x[:4]], 0)
        both = (cov[0:1, lanes] + cov[1:2, lanes]) * f1
        c, s = cos_sin(jnp.broadcast_to(both, (8, 256)))
        xrot[:, lanes] = x * c + swapped * (s * sign)

    loop(0, 16, rotate)

    loop(1, N_STA, lambda d: arrival(r_recv, r_rs, (sj + d) % N_STA).wait())

    @pl.when(half != core)
    def _():
        arrival(r_recv, r_rs, sj).wait()

    acc = None
    for j in range(16):
        lanes = slice(j * 256, j * 256 + 256)
        r = r_recv[j]
        scale = jnp.concatenate(
            [jnp.concatenate([r[:4], r[:4]], 0), jnp.concatenate([r[4:], r[4:]], 0)], 1
        )
        wbuf[:, lanes] = xrot[:, lanes] * scale
        cosx = tabx[0, :, lanes]
        sinx = tabx[1, :, lanes]
        rows = []
        for part in range(2):
            for tab in (cosx, sinx):
                for g in range(4):
                    n = part * 4 + g
                    rows.append((wbuf[n : n + 1, lanes] * tab).astype(jnp.bfloat16))
        v = jnp.concatenate(rows, 0)
        term = lax.dot_general(
            v, taby[:, lanes], (((1,), (1,)), ((), ())), preferred_element_type=jnp.float32
        )
        acc = term if acc is None else acc + term

    lane = lax.broadcasted_iota(jnp.int32, (128, 128), 1)
    m1 = jnp.where(lane < 96, 1.0, -1.0)
    m2 = jnp.where(lane < 32, -1.0, 1.0)
    re = acc[:128] * m1 + pltpu.roll(acc[128:256], 64, 1) * m2
    im = pltpu.roll(acc[256:384] * m1 + pltpu.roll(acc[384:], 64, 1) * m2, 64, 1)
    plus = (re + im) * (re + im)
    minus = (re - im) * (re - im)
    plus = (plus[:32] + plus[32:64]) + (plus[64:96] + plus[96:])
    minus = (minus[:32] + minus[32:64]) + (minus[64:96] + minus[96:])
    grid = plus + pltpu.roll(minus, 64, 1)
    high = grid.astype(jnp.bfloat16)
    low = (grid - high.astype(jnp.float32)).astype(jnp.bfloat16)
    parts = jnp.concatenate([high, low], 0)
    for n in range(0, 2048, 256):
        picked = jnp.dot(parts, pick[:, n : n + 256], preferred_element_type=jnp.float32)
        picked = picked[:32] + picked[32:]
        hot = lax.broadcasted_iota(jnp.int32, (GRID_K, 256), 0) == kx[:, n : n + 256]
        res = jnp.sum(jnp.where(hot, picked, 0.0), 0, keepdims=True)
        pow_send[n // 128] = res[:, :128]
        pow_send[n // 128 + 1] = res[:, 128:]

    loop(1, N_STA, lambda d: pow_copy(d).start())
    pow_recv[sj] = pow_send[sj]
    loop(1, N_STA, lambda d: arrival(pow_recv, pow_rs, (sj + d) % N_STA).wait())
    for b in range(8):
        out_ref[b : b + 1, :] = (pow_recv[2 * b] + pow_recv[2 * b + 1]) * (1.0 / 32768)

    loop(1, N_BINS, lambda d: part_copy(d).wait_send())
    loop(1, N_STA, lambda d: raw_copy(d).wait_send())
    loop(0, 8, lambda e: r_copy(1, e).wait_send())
    loop(1, 8, lambda e: r_copy(0, e).wait_send())

    @pl.when(half != core)
    def _():
        r_copy(0, 0).wait_send()

    loop(1, N_STA, lambda d: pow_copy(d).wait_send())


def local(spectra, coords, slowness):
    f32, bf16, i32 = jnp.float32, jnp.bfloat16, jnp.int32
    dma = pltpu.SemaphoreType.DMA
    return pl.pallas_call(
        kernel,
        out_shape=jax.ShapeDtypeStruct((8, 128), f32),
        in_specs=[pl.BlockSpec(memory_space=pl.ANY)] * 3,
        out_specs=pl.BlockSpec(memory_space=pltpu.VMEM),
        scratch_shapes=[
            pltpu.VMEM((2, 8, 8, 256), bf16),
            pltpu.VMEM((2, 4096), i32),
            pltpu.VMEM((2, 2048), i32),
            pltpu.VMEM((16, 16, 128), bf16),
            pltpu.VMEM((16, 16, 128), bf16),
            pltpu.VMEM((2, 8, 128), f32),
            pltpu.VMEM((16, 8, 128), f32),
            pltpu.VMEM((8, 128), f32),
            pltpu.VMEM((16, 8, 128), f32),
            pltpu.VMEM((16, 1, 128), f32),
            pltpu.VMEM((16, 1, 128), f32),
            pltpu.VMEM((2, GRID_K, 4096), f32),
            pltpu.VMEM((128, 4096), bf16),
            pltpu.VMEM((8, 4096), f32),
            pltpu.VMEM((8, 4096), f32),
            pltpu.VMEM((128, 2048), bf16),
            dma((3,)),
            dma((16,)), dma((16,)), dma((16,)), dma((16,)),
            dma((16,)), dma((16,)), dma((16,)), dma((16,)),
        ],
        compiler_params=pltpu.CompilerParams(collective_id=0, has_side_effects=True),
    )(spectra, coords, slowness)


def solution(mesh):
    in_specs = (P(None, "bins", None, "sta"), P(), P())
    out_specs = P("bins", "sta")
    return jax.shard_map(local, mesh=mesh, in_specs=in_specs, out_specs=out_specs, check_vma=False)
```

time: 147 us -> 33.1 us (0.23)
  other arithmetic: 84.1 us -> 0 us
  Pallas kernels: 0 us -> 31.7 us
  waiting for transfers between devices: 27.5 us -> 0 us
  blocking collectives: 13.1 us -> 0 us
  starting transfers between devices: 10 us -> 0 us
  local copies, waits for them, and re-layouts: 7.81 us -> 1.28 us
  matrix products: 3.16 us -> 0 us
    another operation x9 -> x0, other arithmetic: 80.3 us -> none
    pallas_call x0 -> x1, Pallas kernels: none -> 31.7 us  [local(): pl.pallas_call(kernel, out_shape=jax.ShapeDtypeStruct((8, 128), f32), in_...]
    all_to_all x1 -> x0, waiting for transfers between devices: 27.5 us -> none  [sent_to_all(): lax.all_to_all(jnp.broadcast_to(x[None], (peers, *x.shape)), axis, 0, 0,...]
    all_to_all x1 -> x0, blocking collectives: 13.1 us -> none  [sent_to_all(): lax.all_to_all(jnp.broadcast_to(x[None], (peers, *x.shape)), axis, 0, 0,...]
    all_to_all x1 -> x0, starting transfers between devices: 10 us -> none  [sent_to_all(): lax.all_to_all(jnp.broadcast_to(x[None], (peers, *x.shape)), axis, 0, 0,...]
    dynamic_slice x9 -> x0, local copies, waits for them, and re-layouts: 4.7 us -> none  [the longest x8 4.69 us: one_block(): amps = lax.map(one_bin, (stacked, bin_numbers))]
    dot_general x8 -> x0, matrix products: 3.16 us -> none  [one_bin(): lax.dot_general(steering, bin_rows, (((0,), (1,)), ((), ())), preferred_e...]
  transfers between devices with their start and end apart: 1 -> 0, of which waited for: 1 -> 0; matrix products, arithmetic and copies ran while one was open for 0% -> 0% of each run, Pallas kernels for 0% -> 0%
where the time goes in v1:
time: 33.1 us; the launch traced here: 33 us
  Pallas kernels  31.7 us (96%)
  local copies, waits for them, and re-layouts  1.28 us (4%)
    pallas_call x1, Pallas kernels, local(): pl.pallas_call(kernel, out_shape=jax.ShapeDtypeStruct((8, 128), f32), in_...  31.7 us
    unnamed x1, local copies, waits for them, and re-layouts  1.28 us

profile of v1, /device:TPU:1, one launch (start us, length us, event | category | flops | bytes accessed | tf_op | source)
XLA Modules:
  0.0 33.0 jit_solution(6675080905856056734)
XLA Ops:
  0.0 31.7 %shard_map.37 = f32[8,128]{1,0:T(8,128)} custom-call(bf16[2,8,8,256]{3,2,1,0:T(8,128)(2,1)} %x_hbm.1, s32[2,4096]{1,0:T(2,128)} %co_hbm.1, s32[2,2048]{1,0:T(2,128)} %sl_hbm.1), custom_call_target="tpu_custom_call" | custom-call | tf_op jit(solution)/shard_map/pallas_call | solution.py:281
  31.7 1.3 %copy.5 = f32[8,128]{1,0:T(8,128)} copy(f32[8,128]{1,0:T(8,128)} %shard_map.37) | data formatting | bytes 8192
